TPU v7x, 32 devices: a whole 2x2x4 slice. The times are simulated.
32 devices in a mesh: clip: 4 (over x, core), tx: 4 (over z), ty: 2 (over y).
Axes of the slice: x: 2, y: 2, z: 4, core: 2. Of those that a mesh axis runs over, the one named last changes fastest.
Arguments:
- query_states: bfloat16 [32, 128, 1152], P(('clip', 'tx', 'ty')), parts along dimension 0, may hold values from -64 to 64
- key_states: bfloat16 [32, 128, 1152], P(('clip', 'tx', 'ty')), parts along dimension 0, may hold values from -24 to 24
- value_states: bfloat16 [32, 128, 1152], P(('clip', 'tx', 'ty')), parts along dimension 0, may hold values from -6 to 6
- grad_output: bfloat16 [32, 128, 1152], P(('clip', 'tx', 'ty')), parts along dimension 0, may hold values from -6 to 6
- branch_gate: float32 [4608], P('clip'), parts along dimension 0, may hold values from 0.1 to 1.9
- out_weight: bfloat16 [1152, 1152], P('tx'), may hold values from -0.1875 to 0.1875
Outputs:
- query_grad: bfloat16 [32, 128, 1152], P(('clip', 'tx', 'ty')), parts along dimension 0
- key_grad: bfloat16 [32, 128, 1152], P(('clip', 'tx', 'ty')), parts along dimension 0
- value_grad: bfloat16 [32, 128, 1152], P(('clip', 'tx', 'ty')), parts along dimension 0
- gate_grad: float32 [4608], P('clip'), parts along dimension 0
There are 4 independent parts, one for each index of `clip`. A program takes and returns all parts, laid end to end along the dimension named above; an argument that names none is the same for every part. Nothing has to cross between parts.
All inputs are finite; a program needn't handle non-finite values.
Results may differ from a plain program's by a relative error of at most 0.025.
Values may be sent and summed in bfloat16 or wider, within the bound.
A program may use at most 64 MiB of HBM per device.

v0:
```python
import jax
import jax.numpy as jnp
from jax import lax
from jax.sharding import PartitionSpec as P

HEAD_DIM = 72


def shortened(x):

    def short(part):
        return part.astype(jnp.bfloat16) if part.dtype == jnp.float32 else part

    return jax.tree.map(short, x)


def attend_block(queries, keys_in, values_in, grads_in):
    frames, block_pos, block_width = queries.shape
    heads_here = block_width // HEAD_DIM
    shape4 = (frames, block_pos, heads_here, HEAD_DIM)
    q_four = queries.reshape(shape4)
    k_four = keys_in.reshape(shape4)
    v_four = values_in.reshape(shape4)
    g_four = grads_in.reshape(shape4)
    factor = HEAD_DIM ** (-0.5)
    scores = (
        jnp.einsum("fphd,gphd->phfg", q_four, k_four, preferred_element_type=jnp.float32) * factor
    )
    peak = jnp.max(scores, axis=-1, keepdims=True)
    expon = jnp.exp(scores - peak)
    probs = expon / jnp.sum(expon, axis=-1, keepdims=True)
    probs_b = probs.astype(jnp.bfloat16)
    attn_out = jnp.einsum(
        "phfg,gphd->fphd", probs_b, v_four, preferred_element_type=jnp.float32
    ).astype(jnp.bfloat16)
    value_grad = jnp.einsum(
        "phfg,fphd->gphd", probs_b, g_four, preferred_element_type=jnp.float32
    ).astype(jnp.bfloat16)
    dprobs = jnp.einsum("fphd,gphd->phfg", g_four, v_four, preferred_element_type=jnp.float32)
    delta = jnp.sum(g_four.astype(jnp.float32) * attn_out.astype(jnp.float32), axis=-1)
    delta = jnp.transpose(delta, (1, 2, 0))[..., None]
    dscores = (probs * (dprobs - delta) * factor).astype(jnp.bfloat16)
    query_grad = jnp.einsum(
        "phfg,gphd->fphd", dscores, k_four, preferred_element_type=jnp.float32
    ).astype(jnp.bfloat16)
    key_grad = jnp.einsum(
        "phfg,fphd->gphd", dscores, q_four, preferred_element_type=jnp.float32
    ).astype(jnp.bfloat16)
    flat = (frames, block_pos, block_width)
    return (
        query_grad.reshape(flat),
        key_grad.reshape(flat),
        value_grad.reshape(flat),
        attn_out.reshape(flat),
    )


def split_for_direct(array, across_x, across_y):
    positions, width = array.shape
    pieces = array.reshape(across_y, positions // across_y, across_x, width // across_x)
    pieces = jnp.transpose(pieces, (2, 0, 1, 3))
    return pieces.reshape(1, across_x * across_y, positions // across_y, width // across_x)


def join_from_direct(array, across_x, across_y):
    block_pos, block_width = (array.shape[2], array.shape[3])
    pieces = array.reshape(across_x, across_y, block_pos, block_width)
    pieces = jnp.transpose(pieces, (1, 2, 0, 3))
    return pieces.reshape(1, across_y * block_pos, across_x * block_width)


def per_device(query_states, key_states, value_states, grad_output, branch_gate, out_weight):
    across_x = lax.axis_size("tx")
    across_y = lax.axis_size("ty")
    devices_here = across_x * across_y
    positions = grad_output.shape[1]
    width = grad_output.shape[2]
    block_pos = positions // across_y
    block_width = width // across_x
    grad_rows = grad_output[0]
    gated = (grad_rows.astype(jnp.float32) * branch_gate).astype(jnp.bfloat16)
    d_attn = lax.dot_general(
        gated,
        lax.all_gather(out_weight, "tx", axis=0, tiled=True),
        (((1,), (1,)), ((), ())),
        preferred_element_type=jnp.float32,
    )
    d_attn = d_attn.astype(jnp.bfloat16)
    sources = (query_states[0], key_states[0], value_states[0], d_attn)
    prepared = tuple((split_for_direct(arr, across_x, across_y) for arr in sources))
    moved = jax.tree.map(
        lambda part, own: part.astype(own.dtype),
        lax.all_to_all(shortened(prepared), ("tx", "ty"), split_axis=1, concat_axis=0, tiled=True),
        prepared,
    )
    moved = tuple((arr.reshape(devices_here, block_pos, block_width) for arr in moved))
    results = attend_block(moved[0], moved[1], moved[2], moved[3])
    outgoing = tuple((arr.reshape(devices_here, 1, block_pos, block_width) for arr in results))
    returned = jax.tree.map(
        lambda part, own: part.astype(own.dtype),
        lax.all_to_all(shortened(outgoing), ("tx", "ty"), split_axis=0, concat_axis=1, tiled=True),
        outgoing,
    )
    returned = tuple((join_from_direct(arr, across_x, across_y) for arr in returned))
    query_grad, key_grad, value_grad, attn_frame = returned
    attn_rows = attn_frame[0]
    branch_out = jnp.dot(
        attn_rows,
        lax.all_gather(out_weight, "tx", axis=0, tiled=True),
        preferred_element_type=jnp.float32,
    )
    local_terms = jnp.sum(grad_rows.astype(jnp.float32) * branch_out, axis=0)
    gate_grad = lax.psum(local_terms, ("tx", "ty"))
    return (query_grad, key_grad, value_grad, gate_grad)


def solution(mesh):
    in_specs = (
        P(("clip", "tx", "ty"), None, None),
        P(("clip", "tx", "ty"), None, None),
        P(("clip", "tx", "ty"), None, None),
        P(("clip", "tx", "ty"), None, None),
        P("clip"),
        P("tx", None),
    )
    out_specs = (
        P(("clip", "tx", "ty"), None, None),
        P(("clip", "tx", "ty"), None, None),
        P(("clip", "tx", "ty"), None, None),
        P("clip"),
    )
    return jax.shard_map(
        per_device, mesh=mesh, in_specs=in_specs, out_specs=out_specs, check_vma=False
    )
```

profile of v0, /device:TPU:0, one launch (start us, length us, event | category | flops | bytes accessed | tf_op | source)
XLA Modules:
  0.0 204.5 jit_solution(13158037343326057094)
XLA Ops:
  7.2 0.7 all-gather.2.cloned.1.call-update
  7.9 1.3 reshape_squeeze.9
  9.2 0.8 copy.55
  10.1 7.4 %all-to-all-start = ((bf16[1,8,64,288]{3,2,0,1:T(8,128)(2,1)}), bf16[1,8,64,288]{3,2,0,1:T(8,128)(2,1)S(1)}, u32[]{:S(2)}, u32[]{:S(2)}) async-start(bf16[1,8,64,288]{3,2,0,1:T(8,128)(2,1)} %bitcast.2), calls=%async_computation | async-start | bytes 786432 | tf_op jit(solution)/shard_map/all_to_all | solution.py:93
  17.5 0.4 reshape_squeeze.10
  17.9 0.8 copy.57
  18.7 19.1 %all-to-all-done = bf16[1,8,64,288]{3,2,0,1:T(8,128)(2,1)S(1)} async-done(((bf16[1,8,64,288]{3,2,0,1:T(8,128)(2,1)}), bf16[1,8,64,288]{3,2,0,1:T(8,128)(2,1)S(1)}, u32[]{:S(2)}, u32[]{:S(2)}) %all-to-all-start) | async-done | bytes 294944 | tf_op jit(solution)/shard_map/all_to_all | solution.py:93
  37.8 6.1 %all-to-all-start.1 = ((bf16[1,8,64,288]{3,2,0,1:T(8,128)(2,1)}), bf16[1,8,64,288]{3,2,0,1:T(8,128)(2,1)S(1)}, u32[]{:S(2)}, u32[]{:S(2)}) async-start(bf16[1,8,64,288]{3,2,0,1:T(8,128)(2,1)} %bitcast.5), calls=%async_computation.1 | async-start | bytes 786432 | tf_op jit(solution)/shard_map/all_to_all | solution.py:93
  43.8 0.4 reshape_squeeze.11
  44.2 0.8 copy.63
  45.0 20.7 %all-to-all-done.1 = bf16[1,8,64,288]{3,2,0,1:T(8,128)(2,1)S(1)} async-done(((bf16[1,8,64,288]{3,2,0,1:T(8,128)(2,1)}), bf16[1,8,64,288]{3,2,0,1:T(8,128)(2,1)S(1)}, u32[]{:S(2)}, u32[]{:S(2)}) %all-to-all-start.1) | async-done | bytes 294944 | tf_op jit(solution)/shard_map/all_to_all | solution.py:93
  65.7 3.5 %all-to-all-start.3 = ((bf16[1,8,64,288]{3,2,0,1:T(8,128)(2,1)}), bf16[1,8,64,288]{3,2,0,1:T(8,128)(2,1)S(1)}, u32[]{:S(2)}, u32[]{:S(2)}) async-start(bf16[1,8,64,288]{3,2,0,1:T(8,128)(2,1)} %bitcast.12), calls=%async_computation.3 | async-start | bytes 786432 | tf_op jit(solution)/shard_map/all_to_all | solution.py:93
  69.2 20.1 %all-gather.2.cloned.1.call-done = bf16[1152,1152]{1,0:T(8,128)(2,1)} async-done(((bf16[288,1152]{1,0:T(8,128)(2,1)}), bf16[1152,1152]{1,0:T(8,128)(2,1)}) %all-gather.2.cloned.1.call-update) | async-done | bytes 2654224 | tf_op jit(solution)/shard_map/all_gather | solution.py:84
  89.3 2.7 %convolution_convert_fusion = bf16[128,1152]{1,0:T(8,128)(2,1)S(1)} fusion(bf16[1152,1152]{1,0:T(8,128)(2,1)} %all-gather.2.cloned.1.call-done, bf16[1,128,1152]{2,1,0:T(8,128)(2,1)S(1)} %copy-done.1, f32[1152]{0:T(1024)S(1)} %copy-done.5), kind=kOutput, calls=%fused_computation.2 | convolution fusion | flops 340328448 | bytes 3248640 | tf_op jit(solution)/shard_map/dot_general | solution.py:82
  91.9 0.4 reshape.84
  92.3 0.8 copy.61
  93.1 3.5 %all-to-all-start.2 = ((bf16[1,8,64,288]{3,2,0,1:T(8,128)(2,1)}), bf16[1,8,64,288]{3,2,0,1:T(8,128)(2,1)S(1)}, u32[]{:S(2)}, u32[]{:S(2)}) async-start(bf16[1,8,64,288]{3,2,0,1:T(8,128)(2,1)} %bitcast.9), calls=%async_computation.2 | async-start | bytes 786432 | tf_op jit(solution)/shard_map/all_to_all | solution.py:93
  96.6 0.3 reshape_reshape.24
  97.0 0.3 reshape_reshape.25
  97.3 1.1 reshape_reshape.27
  98.4 2.1 %fusion.36 = (f32[64,4,8]{2,1,0:T(4,128)S(1)}, f32[64,4,8,8]{2,3,1,0:T(8,128)}) fusion(bf16[8,64,4,72]{3,2,1,0:T(4,128)(2,1)S(1)} %reshape_reshape.25, bf16[8,64,4,72]{3,2,1,0:T(4,128)(2,1)S(1)} %reshape_reshape.24), kind=kOutput, calls=%fused_computation.37 | convolution fusion | flops 2408455 | bytes 663552 | tf_op jit(solution)/shard_map/sub | solution.py:30
  100.5 8.1 %all-to-all-done.2 = bf16[1,8,64,288]{3,2,0,1:T(8,128)(2,1)S(1)} async-done(((bf16[1,8,64,288]{3,2,0,1:T(8,128)(2,1)}), bf16[1,8,64,288]{3,2,0,1:T(8,128)(2,1)S(1)}, u32[]{:S(2)}, u32[]{:S(2)}) %all-to-all-start.2) | async-done | bytes 294944 | tf_op jit(solution)/shard_map/all_to_all | solution.py:93
  108.6 0.3 reshape_reshape.26
  109.0 3.1 %multiply_reduce_fusion = (f32[8,64,4]{0,2,1:T(4,128)S(1)}, bf16[8,64,4,72]{3,0,2,1:T(8,128)(2,1)}) fusion(bf16[8,64,4,72]{3,2,1,0:T(4,128)(2,1)S(1)} %reshape_reshape.26, bf16[8,64,4,72]{3,2,1,0:T(4,128)(2,1)} %reshape_reshape.27, f32[64,4,8,8]{2,3,1,0:T(8,128)} %get-tuple-element.5, f32[64,4,8]{2,1,0:T(4,128)S(1)} %get-tuple-element.4), kind=kOutput, calls=%fused_computation.19 | convolution fusion | flops 3127296 | bytes 966656 | tf_op jit(solution)/shard_map/phfg,gphd->fphd/dot_general | solution.py:33
  112.1 0.8 fusion.5
  112.9 0.5 fusion.8
  113.6 1.1 reshape_reshape.29
  114.7 3.6 %all-to-all-start.5 = ((bf16[8,1,64,288]{3,2,1,0:T(8,128)(2,1)}), bf16[8,1,64,288]{3,2,1,0:T(8,128)(2,1)S(1)}, u32[]{:S(2)}, u32[]{:S(2)}) async-start(bf16[8,1,64,288]{3,2,1,0:T(8,128)(2,1)} %bitcast.20), calls=%async_computation.5 | async-start | bytes 786432 | tf_op jit(solution)/shard_map/all_to_all | solution.py:101
  118.3 0.5 fusion.7
  119.1 1.1 reshape_reshape.28
  120.2 10.0 %all-to-all-done.5 = bf16[8,1,64,288]{3,2,1,0:T(8,128)(2,1)S(1)} async-done(((bf16[8,1,64,288]{3,2,1,0:T(8,128)(2,1)}), bf16[8,1,64,288]{3,2,1,0:T(8,128)(2,1)S(1)}, u32[]{:S(2)}, u32[]{:S(2)}) %all-to-all-start.5) | async-done | bytes 294944 | tf_op jit(solution)/shard_map/all_to_all | solution.py:101
  130.2 3.6 %all-to-all-start.4 = ((bf16[8,1,64,288]{3,2,1,0:T(8,128)(2,1)}), bf16[8,1,64,288]{3,2,1,0:T(8,128)(2,1)S(1)}, u32[]{:S(2)}, u32[]{:S(2)}) async-start(bf16[8,1,64,288]{3,2,1,0:T(8,128)(2,1)} %bitcast.16), calls=%async_computation.4 | async-start | bytes 786432 | tf_op jit(solution)/shard_map/all_to_all | solution.py:101
  133.8 1.2 copy.84
  135.1 1.1 reshape_reshape.31
  136.2 9.4 %all-to-all-done.4 = bf16[8,1,64,288]{3,2,1,0:T(8,128)(2,1)S(1)} async-done(((bf16[8,1,64,288]{3,2,1,0:T(8,128)(2,1)}), bf16[8,1,64,288]{3,2,1,0:T(8,128)(2,1)S(1)}, u32[]{:S(2)}, u32[]{:S(2)}) %all-to-all-start.4) | async-done | bytes 294944 | tf_op jit(solution)/shard_map/all_to_all | solution.py:101
  145.6 4.1 %all-to-all-start.7 = ((bf16[8,1,64,288]{3,2,1,0:T(8,128)(2,1)}), bf16[8,1,64,288]{3,2,1,0:T(8,128)(2,1)}, u32[]{:S(2)}, u32[]{:S(2)}) async-start(bf16[8,1,64,288]{3,2,1,0:T(8,128)(2,1)} %bitcast.28), calls=%async_computation.7 | async-start | bytes 786432 | tf_op jit(solution)/shard_map/all_to_all | solution.py:101
  149.7 1.8 fusion.9
  151.7 1.1 reshape_reshape.30
  152.8 8.3 %all-to-all-done.7 = bf16[8,1,64,288]{3,2,1,0:T(8,128)(2,1)} async-done(((bf16[8,1,64,288]{3,2,1,0:T(8,128)(2,1)}), bf16[8,1,64,288]{3,2,1,0:T(8,128)(2,1)}, u32[]{:S(2)}, u32[]{:S(2)}) %all-to-all-start.7) | async-done | bytes 294944 | tf_op jit(solution)/shard_map/all_to_all | solution.py:101
  161.1 4.3 %all-to-all-start.6 = ((bf16[8,1,64,288]{3,2,1,0:T(8,128)(2,1)}), bf16[8,1,64,288]{3,2,1,0:T(8,128)(2,1)}, u32[]{:S(2)}, u32[]{:S(2)}) async-start(bf16[8,1,64,288]{3,2,1,0:T(8,128)(2,1)} %bitcast.73), calls=%async_computation.6 | async-start | bytes 786432 | tf_op jit(solution)/shard_map/all_to_all | solution.py:101
  165.4 1.1 copy.79
  166.4 2.0 %reshape.90 = bf16[1,128,1152]{2,1,0:T(8,128)(2,1)} reshape(bf16[2,64,4,288]{3,2,1,0:T(4,128)(2,1)} %copy.79) | data formatting | bytes 589824 | tf_op jit(solution)/shard_map/reshape | solution.py:69
  168.8 1.0 reshape.88
  169.8 1.3 copy.122
  171.4 1.6 fusion.10
  172.9 22.4 %psum.7 = f32[1152]{0:T(1024)} all-reduce(f32[1152]{0:T(1024)S(1)} %fusion.10), channel_id=1, replica_groups=mesh['clip'=4,'tx'=4,'ty'=2] {'tx','ty'}, use_global_device_ids=true, to_apply=%region_4.0 | all-reduce | flops 1152 | bytes 9216 | tf_op jit(solution)/shard_map/psum | solution.py:113
  195.4 1.3 copy.83
  196.7 1.0 reshape.92
  (22 shorter events, 1.3 us)
Async XLA Ops:
  7.2 10.3 %copy-start.3 = (bf16[1,128,1152]{2,1,0:T(8,128)(2,1)S(1)}, bf16[1,128,1152]{2,1,0:T(8,128)(2,1)}, u32[]{:S(2)}) copy-start(bf16[1,128,1152]{2,1,0:T(8,128)(2,1)} %param.7) | copy-start | bytes 884740
  7.2 36.7 %copy-start.4 = (bf16[1,128,1152]{2,1,0:T(8,128)(2,1)S(1)}, bf16[1,128,1152]{2,1,0:T(8,128)(2,1)}, u32[]{:S(2)}) copy-start(bf16[1,128,1152]{2,1,0:T(8,128)(2,1)} %param.8) | copy-start | bytes 884740
  7.2 82.1 %all-gather.2.cloned.1.call-start = ((), (), s32[]{:S(2)}) async-start(), calls=%async_computation.8 | async-start | bytes 3317760 | tf_op jit(solution)/shard_map/all_gather | solution.py:84
  10.1 79.2 %copy-start.1 = (bf16[1,128,1152]{2,1,0:T(8,128)(2,1)S(1)}, bf16[1,128,1152]{2,1,0:T(8,128)(2,1)}, u32[]{:S(2)}) copy-start(bf16[1,128,1152]{2,1,0:T(8,128)(2,1)} %param.9) | copy-start | bytes 884740
  10.1 79.2 %copy-start.5 = (f32[1152]{0:T(1024)S(1)}, f32[1152]{0:T(1024)}, u32[]{:S(2)}) copy-start(f32[1152]{0:T(1024)} %param.10) | copy-start | bytes 13828
  10.1 27.7 %all-to-all-start = ((bf16[1,8,64,288]{3,2,0,1:T(8,128)(2,1)}), bf16[1,8,64,288]{3,2,0,1:T(8,128)(2,1)S(1)}, u32[]{:S(2)}, u32[]{:S(2)}) async-start(bf16[1,8,64,288]{3,2,0,1:T(8,128)(2,1)} %bitcast.2), calls=%async_computation | async-start | bytes 786432 | tf_op jit(solution)/shard_map/all_to_all | solution.py:93
  37.8 28.0 %all-to-all-start.1 = ((bf16[1,8,64,288]{3,2,0,1:T(8,128)(2,1)}), bf16[1,8,64,288]{3,2,0,1:T(8,128)(2,1)S(1)}, u32[]{:S(2)}, u32[]{:S(2)}) async-start(bf16[1,8,64,288]{3,2,0,1:T(8,128)(2,1)} %bitcast.5), calls=%async_computation.1 | async-start | bytes 786432 | tf_op jit(solution)/shard_map/all_to_all | solution.py:93
  65.7 27.4 %all-to-all-start.3 = ((bf16[1,8,64,288]{3,2,0,1:T(8,128)(2,1)}), bf16[1,8,64,288]{3,2,0,1:T(8,128)(2,1)S(1)}, u32[]{:S(2)}, u32[]{:S(2)}) async-start(bf16[1,8,64,288]{3,2,0,1:T(8,128)(2,1)} %bitcast.12), calls=%async_computation.3 | async-start | bytes 786432 | tf_op jit(solution)/shard_map/all_to_all | solution.py:93
  93.1 15.5 %all-to-all-start.2 = ((bf16[1,8,64,288]{3,2,0,1:T(8,128)(2,1)}), bf16[1,8,64,288]{3,2,0,1:T(8,128)(2,1)S(1)}, u32[]{:S(2)}, u32[]{:S(2)}) async-start(bf16[1,8,64,288]{3,2,0,1:T(8,128)(2,1)} %bitcast.9), calls=%async_computation.2 | async-start | bytes 786432 | tf_op jit(solution)/shard_map/all_to_all | solution.py:93
  108.9 3.1 %copy-start.2 = (bf16[8,64,4,72]{3,2,1,0:T(4,128)(2,1)S(1)}, bf16[8,64,4,72]{3,2,1,0:T(4,128)(2,1)}, u32[]{:S(2)}) copy-start(bf16[8,64,4,72]{3,2,1,0:T(4,128)(2,1)} %reshape_reshape.27) | copy-start | bytes 884740
  108.9 3.1 %copy-start.6 = (f32[64,4,8,8]{2,3,1,0:T(8,128)S(1)}, f32[64,4,8,8]{2,3,1,0:T(8,128)}, u32[]{:S(2)}) copy-start(f32[64,4,8,8]{2,3,1,0:T(8,128)} %get-tuple-element.5) | copy-start | bytes 196612
  114.7 15.5 %all-to-all-start.5 = ((bf16[8,1,64,288]{3,2,1,0:T(8,128)(2,1)}), bf16[8,1,64,288]{3,2,1,0:T(8,128)(2,1)S(1)}, u32[]{:S(2)}, u32[]{:S(2)}) async-start(bf16[8,1,64,288]{3,2,1,0:T(8,128)(2,1)} %bitcast.20), calls=%async_computation.5 | async-start | bytes 786432 | tf_op jit(solution)/shard_map/all_to_all | solution.py:101
  130.2 15.4 %all-to-all-start.4 = ((bf16[8,1,64,288]{3,2,1,0:T(8,128)(2,1)}), bf16[8,1,64,288]{3,2,1,0:T(8,128)(2,1)S(1)}, u32[]{:S(2)}, u32[]{:S(2)}) async-start(bf16[8,1,64,288]{3,2,1,0:T(8,128)(2,1)} %bitcast.16), calls=%async_computation.4 | async-start | bytes 786432 | tf_op jit(solution)/shard_map/all_to_all | solution.py:101
  145.6 15.5 %all-to-all-start.7 = ((bf16[8,1,64,288]{3,2,1,0:T(8,128)(2,1)}), bf16[8,1,64,288]{3,2,1,0:T(8,128)(2,1)}, u32[]{:S(2)}, u32[]{:S(2)}) async-start(bf16[8,1,64,288]{3,2,1,0:T(8,128)(2,1)} %bitcast.28), calls=%async_computation.7 | async-start | bytes 786432 | tf_op jit(solution)/shard_map/all_to_all | solution.py:101
  152.8 18.6 %copy-start = (bf16[1152,1152]{1,0:T(8,128)(2,1)S(1)}, bf16[1152,1152]{1,0:T(8,128)(2,1)}, u32[]{:S(2)}) copy-start(bf16[1152,1152]{1,0:T(8,128)(2,1)} %all-gather.2.cloned.1.call-done) | copy-start | bytes 7962628
  161.1 34.3 %all-to-all-start.6 = ((bf16[8,1,64,288]{3,2,1,0:T(8,128)(2,1)}), bf16[8,1,64,288]{3,2,1,0:T(8,128)(2,1)}, u32[]{:S(2)}, u32[]{:S(2)}) async-start(bf16[8,1,64,288]{3,2,1,0:T(8,128)(2,1)} %bitcast.73), calls=%async_computation.6 | async-start | bytes 786432 | tf_op jit(solution)/shard_map/all_to_all | solution.py:101
Sparse Core Ops, SparseCore 0:
  9.6 79.6 all-gather.1
where the time goes:
time: 206 us; the launch traced here: 205 us
  waiting for transfers between devices  96.3 us (47%)
  starting transfers between devices  36.2 us (18%)
  blocking collectives  22.4 us (11%)
  local copies, waits for them, and re-layouts  22.3 us (11%)
  between operations  14.2 us (7%)
  matrix products  13 us (6%)
    all_to_all x4, waiting for transfers between devices, per_device(): lax.all_to_all(shortened(prepared), ('tx', 'ty'), split_axis=1, concat_ax...  47.9 us
    all_to_all x4, waiting for transfers between devices, per_device(): lax.all_to_all(shortened(outgoing), ('tx', 'ty'), split_axis=0, concat_ax...  27.7 us
    psum x1, blocking collectives, per_device(): gate_grad = lax.psum(local_terms, ('tx', 'ty'))  22.4 us
    all_to_all x4, starting transfers between devices, per_device(): lax.all_to_all(shortened(prepared), ('tx', 'ty'), split_axis=1, concat_ax...  20.5 us
    all_gather x1, waiting for transfers between devices, per_device(): lax.all_gather(out_weight, 'tx', axis=0, tiled=True)  20.1 us
    all_to_all x4, starting transfers between devices, per_device(): lax.all_to_all(shortened(outgoing), ('tx', 'ty'), split_axis=0, concat_ax...  15.6 us
    another operation x4, local copies, waits for them, and re-layouts, per_device(): arr.reshape(devices_here, 1, block_pos, block_width)  4.46 us
  transfers between devices with their start and end apart: 9, of which 7 were waited for; matrix products, arithmetic and copies ran while one was open for 13% of the time, Pallas kernels for 0%

commit v1 on v0

--- a/solution.py
+++ b/solution.py
@@ -110,7 +110,7 @@
         preferred_element_type=jnp.float32,
     )
     local_terms = jnp.sum(grad_rows.astype(jnp.float32) * branch_out, axis=0)
-    gate_grad = lax.psum(local_terms, ("tx", "ty"))
+    gate_grad = jnp.sum(lax.all_gather(local_terms, ("tx", "ty")), axis=0)
     return (query_grad, key_grad, value_grad, gate_grad)
 
 

time: 206 us -> 215 us (1.044)
  blocking collectives: 22.4 us -> 31 us
    all_gather x0 -> x1, blocking collectives: none -> 31 us  [per_device(): gate_grad = jnp.sum(lax.all_gather(local_terms, ('tx', 'ty')), axis=0)]
    psum x1 -> x0, blocking collectives: 22.4 us -> none  [per_device(): gate_grad = lax.psum(local_terms, ('tx', 'ty'))]
  transfers between devices with their start and end apart: 9 -> 9, of which waited for: 7 -> 7; matrix products, arithmetic and copies ran while one was open for 13% -> 12% of each run, Pallas kernels for 0% -> 0%
where the time goes in v1:
time: 215 us; the launch traced here: 214 us
  waiting for transfers between devices  97 us (45%)
  starting transfers between devices  36.2 us (17%)
  blocking collectives  31 us (14%)
  local copies, waits for them, and re-layouts  21.6 us (10%)
  between operations  14.2 us (7%)
  matrix products  12.9 us (6%)
    all_to_all x4, waiting for transfers between devices, per_device(): lax.all_to_all(shortened(prepared), ('tx', 'ty'), split_axis=1, concat_ax...  48.7 us
    all_gather x1, blocking collectives, per_device(): gate_grad = jnp.sum(lax.all_gather(local_terms, ('tx', 'ty')), axis=0)  31 us
    all_to_all x4, waiting for transfers between devices, per_device(): lax.all_to_all(shortened(outgoing), ('tx', 'ty'), split_axis=0, concat_ax...  27.6 us
    all_to_all x4, starting transfers between devices, per_device(): lax.all_to_all(shortened(prepared), ('tx', 'ty'), split_axis=1, concat_ax...  20.5 us
    all_gather x1, waiting for transfers between devices, per_device(): lax.all_gather(out_weight, 'tx', axis=0, tiled=True)  20.1 us
    all_to_all x4, starting transfers between devices, per_device(): lax.all_to_all(shortened(outgoing), ('tx', 'ty'), split_axis=0, concat_ax...  15.6 us
    another operation x4, local copies, waits for them, and re-layouts, per_device(): arr.reshape(devices_here, 1, block_pos, block_width)  4.49 us
  transfers between devices with their start and end apart: 9, of which 7 were waited for; matrix products, arithmetic and copies ran while one was open for 12% of the time, Pallas kernels for 0%

profile of v1, /device:TPU:0, one launch (start us, length us, event | category | flops | bytes accessed | tf_op | source)
XLA Modules:
  0.0 213.6 jit_solution(14213414870181917854)
XLA Ops:
  7.2 0.7 all-gather.4.cloned.1.call-update
  7.9 1.3 reshape_squeeze.9
  9.2 0.8 copy.55
  10.1 7.4 %all-to-all-start = ((bf16[1,8,64,288]{3,2,0,1:T(8,128)(2,1)}), bf16[1,8,64,288]{3,2,0,1:T(8,128)(2,1)S(1)}, u32[]{:S(2)}, u32[]{:S(2)}) async-start(bf16[1,8,64,288]{3,2,0,1:T(8,128)(2,1)} %bitcast.2), calls=%async_computation | async-start | bytes 786432 | tf_op jit(solution)/shard_map/all_to_all | solution.py:93
  17.5 0.4 reshape_squeeze.10
  17.9 0.8 copy.57
  18.7 19.1 %all-to-all-done = bf16[1,8,64,288]{3,2,0,1:T(8,128)(2,1)S(1)} async-done(((bf16[1,8,64,288]{3,2,0,1:T(8,128)(2,1)}), bf16[1,8,64,288]{3,2,0,1:T(8,128)(2,1)S(1)}, u32[]{:S(2)}, u32[]{:S(2)}) %all-to-all-start) | async-done | bytes 294944 | tf_op jit(solution)/shard_map/all_to_all | solution.py:93
  37.8 6.1 %all-to-all-start.1 = ((bf16[1,8,64,288]{3,2,0,1:T(8,128)(2,1)}), bf16[1,8,64,288]{3,2,0,1:T(8,128)(2,1)S(1)}, u32[]{:S(2)}, u32[]{:S(2)}) async-start(bf16[1,8,64,288]{3,2,0,1:T(8,128)(2,1)} %bitcast.5), calls=%async_computation.1 | async-start | bytes 786432 | tf_op jit(solution)/shard_map/all_to_all | solution.py:93
  43.9 0.4 reshape_squeeze.11
  44.2 0.8 copy.63
  45.1 20.7 %all-to-all-done.1 = bf16[1,8,64,288]{3,2,0,1:T(8,128)(2,1)S(1)} async-done(((bf16[1,8,64,288]{3,2,0,1:T(8,128)(2,1)}), bf16[1,8,64,288]{3,2,0,1:T(8,128)(2,1)S(1)}, u32[]{:S(2)}, u32[]{:S(2)}) %all-to-all-start.1) | async-done | bytes 294944 | tf_op jit(solution)/shard_map/all_to_all | solution.py:93
  65.8 3.5 %all-to-all-start.3 = ((bf16[1,8,64,288]{3,2,0,1:T(8,128)(2,1)}), bf16[1,8,64,288]{3,2,0,1:T(8,128)(2,1)S(1)}, u32[]{:S(2)}, u32[]{:S(2)}) async-start(bf16[1,8,64,288]{3,2,0,1:T(8,128)(2,1)} %bitcast.12), calls=%async_computation.3 | async-start | bytes 786432 | tf_op jit(solution)/shard_map/all_to_all | solution.py:93
  69.2 20.1 %all-gather.4.cloned.1.call-done = bf16[1152,1152]{1,0:T(8,128)(2,1)} async-done(((bf16[288,1152]{1,0:T(8,128)(2,1)}), bf16[1152,1152]{1,0:T(8,128)(2,1)}) %all-gather.4.cloned.1.call-update) | async-done | bytes 2654224 | tf_op jit(solution)/shard_map/all_gather | solution.py:84
  89.3 2.7 %convolution_convert_fusion = bf16[128,1152]{1,0:T(8,128)(2,1)S(1)} fusion(bf16[1152,1152]{1,0:T(8,128)(2,1)} %all-gather.4.cloned.1.call-done, bf16[1,128,1152]{2,1,0:T(8,128)(2,1)S(1)} %copy-done.1, f32[1152]{0:T(1024)S(1)} %copy-done.4), kind=kOutput, calls=%fused_computation.2 | convolution fusion | flops 340328448 | bytes 3248640 | tf_op jit(solution)/shard_map/dot_general | solution.py:82
  92.0 0.4 reshape.84
  92.3 0.8 copy.61
  93.1 3.5 %all-to-all-start.2 = ((bf16[1,8,64,288]{3,2,0,1:T(8,128)(2,1)}), bf16[1,8,64,288]{3,2,0,1:T(8,128)(2,1)S(1)}, u32[]{:S(2)}, u32[]{:S(2)}) async-start(bf16[1,8,64,288]{3,2,0,1:T(8,128)(2,1)} %bitcast.9), calls=%async_computation.2 | async-start | bytes 786432 | tf_op jit(solution)/shard_map/all_to_all | solution.py:93
  97.0 0.3 reshape_reshape.25
  97.3 0.3 reshape_reshape.27
  97.7 2.1 fusion.36
  99.8 8.8 %all-to-all-done.2 = bf16[1,8,64,288]{3,2,0,1:T(8,128)(2,1)S(1)} async-done(((bf16[1,8,64,288]{3,2,0,1:T(8,128)(2,1)}), bf16[1,8,64,288]{3,2,0,1:T(8,128)(2,1)S(1)}, u32[]{:S(2)}, u32[]{:S(2)}) %all-to-all-start.2) | async-done | bytes 294944 | tf_op jit(solution)/shard_map/all_to_all | solution.py:93
  108.6 0.3 reshape_reshape.26
  109.0 2.9 %multiply_reduce_fusion = (f32[8,64,4]{0,2,1:T(4,128)S(1)}, bf16[8,64,4,72]{3,0,2,1:T(8,128)(2,1)}) fusion(bf16[8,64,4,72]{3,2,1,0:T(4,128)(2,1)S(1)} %reshape_reshape.26, bf16[8,64,4,72]{3,2,1,0:T(4,128)(2,1)S(1)} %reshape_reshape.27, f32[64,4,8,8]{2,3,1,0:T(8,128)} %get-tuple-element.5, f32[64,4,8]{2,1,0:T(4,128)S(1)} %get-tuple-element.4), kind=kOutput, calls=%fused_computation.19 | convolution fusion | flops 3127296 | bytes 966656 | tf_op jit(solution)/shard_map/phfg,gphd->fphd/dot_general | solution.py:33
  111.9 0.9 fusion.5
  112.8 0.5 fusion.8
  113.5 1.1 reshape_reshape.29
  114.6 3.6 %all-to-all-start.5 = ((bf16[8,1,64,288]{3,2,1,0:T(8,128)(2,1)}), bf16[8,1,64,288]{3,2,1,0:T(8,128)(2,1)S(1)}, u32[]{:S(2)}, u32[]{:S(2)}) async-start(bf16[8,1,64,288]{3,2,1,0:T(8,128)(2,1)} %bitcast.20), calls=%async_computation.5 | async-start | bytes 786432 | tf_op jit(solution)/shard_map/all_to_all | solution.py:101
  118.2 0.5 fusion.7
  118.9 1.1 reshape_reshape.28
  120.1 10.0 %all-to-all-done.5 = bf16[8,1,64,288]{3,2,1,0:T(8,128)(2,1)S(1)} async-done(((bf16[8,1,64,288]{3,2,1,0:T(8,128)(2,1)}), bf16[8,1,64,288]{3,2,1,0:T(8,128)(2,1)S(1)}, u32[]{:S(2)}, u32[]{:S(2)}) %all-to-all-start.5) | async-done | bytes 294944 | tf_op jit(solution)/shard_map/all_to_all | solution.py:101
  130.0 3.6 %all-to-all-start.4 = ((bf16[8,1,64,288]{3,2,1,0:T(8,128)(2,1)}), bf16[8,1,64,288]{3,2,1,0:T(8,128)(2,1)S(1)}, u32[]{:S(2)}, u32[]{:S(2)}) async-start(bf16[8,1,64,288]{3,2,1,0:T(8,128)(2,1)} %bitcast.16), calls=%async_computation.4 | async-start | bytes 786432 | tf_op jit(solution)/shard_map/all_to_all | solution.py:101
  133.7 1.2 copy.84
  134.9 1.1 reshape_reshape.31
  136.0 9.4 %all-to-all-done.4 = bf16[8,1,64,288]{3,2,1,0:T(8,128)(2,1)S(1)} async-done(((bf16[8,1,64,288]{3,2,1,0:T(8,128)(2,1)}), bf16[8,1,64,288]{3,2,1,0:T(8,128)(2,1)S(1)}, u32[]{:S(2)}, u32[]{:S(2)}) %all-to-all-start.4) | async-done | bytes 294944 | tf_op jit(solution)/shard_map/all_to_all | solution.py:101
  145.5 4.1 %all-to-all-start.7 = ((bf16[8,1,64,288]{3,2,1,0:T(8,128)(2,1)}), bf16[8,1,64,288]{3,2,1,0:T(8,128)(2,1)}, u32[]{:S(2)}, u32[]{:S(2)}) async-start(bf16[8,1,64,288]{3,2,1,0:T(8,128)(2,1)} %bitcast.28), calls=%async_computation.7 | async-start | bytes 786432 | tf_op jit(solution)/shard_map/all_to_all | solution.py:101
  149.6 1.8 fusion.9
  151.5 1.1 reshape_reshape.30
  152.7 8.2 %all-to-all-done.7 = bf16[8,1,64,288]{3,2,1,0:T(8,128)(2,1)} async-done(((bf16[8,1,64,288]{3,2,1,0:T(8,128)(2,1)}), bf16[8,1,64,288]{3,2,1,0:T(8,128)(2,1)}, u32[]{:S(2)}, u32[]{:S(2)}) %all-to-all-start.7) | async-done | bytes 294944 | tf_op jit(solution)/shard_map/all_to_all | solution.py:101
  160.9 4.3 %all-to-all-start.6 = ((bf16[8,1,64,288]{3,2,1,0:T(8,128)(2,1)}), bf16[8,1,64,288]{3,2,1,0:T(8,128)(2,1)}, u32[]{:S(2)}, u32[]{:S(2)}) async-start(bf16[8,1,64,288]{3,2,1,0:T(8,128)(2,1)} %bitcast.73), calls=%async_computation.6 | async-start | bytes 786432 | tf_op jit(solution)/shard_map/all_to_all | solution.py:101
  165.2 1.1 copy.79
  166.3 2.0 reshape.90
  168.6 1.0 reshape.88
  169.6 1.3 copy.122
  171.2 1.6 fusion.10
  172.8 31.0 %all-gather.1 = f32[8,1,1152]{2,1,0:T(1,128)S(1)} all-gather(f32[1,1,1152]{2,1,0:T(1,128)S(1)} %reshape.96), channel_id=2, replica_groups=mesh['clip'=4,'tx'=4,'ty'=2] {'tx','ty'}, dimensions={0}, use_global_device_ids=true | all-gather | bytes 41472 | tf_op jit(solution)/shard_map/all_gather | solution.py:113
  203.8 1.3 copy.83
  205.1 1.0 reshape.92
  206.1 0.6 reduce_sum.39
  (22 shorter events, 1.6 us)
Async XLA Ops:
  7.2 10.4 %copy-start.2 = (bf16[1,128,1152]{2,1,0:T(8,128)(2,1)S(1)}, bf16[1,128,1152]{2,1,0:T(8,128)(2,1)}, u32[]{:S(2)}) copy-start(bf16[1,128,1152]{2,1,0:T(8,128)(2,1)} %param.7) | copy-start | bytes 884740
  7.2 36.7 %copy-start.3 = (bf16[1,128,1152]{2,1,0:T(8,128)(2,1)S(1)}, bf16[1,128,1152]{2,1,0:T(8,128)(2,1)}, u32[]{:S(2)}) copy-start(bf16[1,128,1152]{2,1,0:T(8,128)(2,1)} %param.8) | copy-start | bytes 884740
  7.2 82.1 %all-gather.4.cloned.1.call-start = ((), (), s32[]{:S(2)}) async-start(), calls=%async_computation.8 | async-start | bytes 3317760 | tf_op jit(solution)/shard_map/all_gather | solution.py:84
  10.1 79.2 %copy-start.1 = (bf16[1,128,1152]{2,1,0:T(8,128)(2,1)S(1)}, bf16[1,128,1152]{2,1,0:T(8,128)(2,1)}, u32[]{:S(2)}) copy-start(bf16[1,128,1152]{2,1,0:T(8,128)(2,1)} %param.9) | copy-start | bytes 884740
  10.1 79.2 %copy-start.4 = (f32[1152]{0:T(1024)S(1)}, f32[1152]{0:T(1024)}, u32[]{:S(2)}) copy-start(f32[1152]{0:T(1024)} %param.10) | copy-start | bytes 13828
  10.1 27.7 %all-to-all-start = ((bf16[1,8,64,288]{3,2,0,1:T(8,128)(2,1)}), bf16[1,8,64,288]{3,2,0,1:T(8,128)(2,1)S(1)}, u32[]{:S(2)}, u32[]{:S(2)}) async-start(bf16[1,8,64,288]{3,2,0,1:T(8,128)(2,1)} %bitcast.2), calls=%async_computation | async-start | bytes 786432 | tf_op jit(solution)/shard_map/all_to_all | solution.py:93
  37.8 28.0 %all-to-all-start.1 = ((bf16[1,8,64,288]{3,2,0,1:T(8,128)(2,1)}), bf16[1,8,64,288]{3,2,0,1:T(8,128)(2,1)S(1)}, u32[]{:S(2)}, u32[]{:S(2)}) async-start(bf16[1,8,64,288]{3,2,0,1:T(8,128)(2,1)} %bitcast.5), calls=%async_computation.1 | async-start | bytes 786432 | tf_op jit(solution)/shard_map/all_to_all | solution.py:93
  65.8 27.4 %all-to-all-start.3 = ((bf16[1,8,64,288]{3,2,0,1:T(8,128)(2,1)}), bf16[1,8,64,288]{3,2,0,1:T(8,128)(2,1)S(1)}, u32[]{:S(2)}, u32[]{:S(2)}) async-start(bf16[1,8,64,288]{3,2,0,1:T(8,128)(2,1)} %bitcast.12), calls=%async_computation.3 | async-start | bytes 786432 | tf_op jit(solution)/shard_map/all_to_all | solution.py:93
  93.1 15.5 %all-to-all-start.2 = ((bf16[1,8,64,288]{3,2,0,1:T(8,128)(2,1)}), bf16[1,8,64,288]{3,2,0,1:T(8,128)(2,1)S(1)}, u32[]{:S(2)}, u32[]{:S(2)}) async-start(bf16[1,8,64,288]{3,2,0,1:T(8,128)(2,1)} %bitcast.9), calls=%async_computation.2 | async-start | bytes 786432 | tf_op jit(solution)/shard_map/all_to_all | solution.py:93
  109.0 3.0 %copy-start.5 = (f32[64,4,8,8]{2,3,1,0:T(8,128)S(1)}, f32[64,4,8,8]{2,3,1,0:T(8,128)}, u32[]{:S(2)}) copy-start(f32[64,4,8,8]{2,3,1,0:T(8,128)} %get-tuple-element.5) | copy-start | bytes 196612
  114.6 15.5 %all-to-all-start.5 = ((bf16[8,1,64,288]{3,2,1,0:T(8,128)(2,1)}), bf16[8,1,64,288]{3,2,1,0:T(8,128)(2,1)S(1)}, u32[]{:S(2)}, u32[]{:S(2)}) async-start(bf16[8,1,64,288]{3,2,1,0:T(8,128)(2,1)} %bitcast.20), calls=%async_computation.5 | async-start | bytes 786432 | tf_op jit(solution)/shard_map/all_to_all | solution.py:101
  130.0 15.4 %all-to-all-start.4 = ((bf16[8,1,64,288]{3,2,1,0:T(8,128)(2,1)}), bf16[8,1,64,288]{3,2,1,0:T(8,128)(2,1)S(1)}, u32[]{:S(2)}, u32[]{:S(2)}) async-start(bf16[8,1,64,288]{3,2,1,0:T(8,128)(2,1)} %bitcast.16), calls=%async_computation.4 | async-start | bytes 786432 | tf_op jit(solution)/shard_map/all_to_all | solution.py:101
  145.5 15.5 %all-to-all-start.7 = ((bf16[8,1,64,288]{3,2,1,0:T(8,128)(2,1)}), bf16[8,1,64,288]{3,2,1,0:T(8,128)(2,1)}, u32[]{:S(2)}, u32[]{:S(2)}) async-start(bf16[8,1,64,288]{3,2,1,0:T(8,128)(2,1)} %bitcast.28), calls=%async_computation.7 | async-start | bytes 786432 | tf_op jit(solution)/shard_map/all_to_all | solution.py:101
  152.7 18.5 %copy-start = (bf16[1152,1152]{1,0:T(8,128)(2,1)S(1)}, bf16[1152,1152]{1,0:T(8,128)(2,1)}, u32[]{:S(2)}) copy-start(bf16[1152,1152]{1,0:T(8,128)(2,1)} %all-gather.4.cloned.1.call-done) | copy-start | bytes 7962628
  160.9 42.9 %all-to-all-start.6 = ((bf16[8,1,64,288]{3,2,1,0:T(8,128)(2,1)}), bf16[8,1,64,288]{3,2,1,0:T(8,128)(2,1)}, u32[]{:S(2)}, u32[]{:S(2)}) async-start(bf16[8,1,64,288]{3,2,1,0:T(8,128)(2,1)} %bitcast.73), calls=%async_computation.6 | async-start | bytes 786432 | tf_op jit(solution)/shard_map/all_to_all | solution.py:101
Sparse Core Ops, SparseCore 0:
  9.6 79.6 all-gather.3
